TPU v7x, 256 devices: a whole 4x4x8 slice. The times are simulated.
256 devices in a mesh: ep: 64 (over z, x, core), tp: 4 (over y).
Axes of the slice: x: 4, y: 4, z: 8, core: 2. Of those that a mesh axis runs over, the one named last changes fastest.
Arguments:
- tokens: bfloat16 [16384, 2048], P('ep', 'tp'), may hold values from -180 to 180
- norm_gain: float32 [2048], replicated, may hold values from 0.1 to 1.9
- router_weight: bfloat16 [2048, 60], P('tp'), may hold values from -2 to 2
- shared_gate_w: bfloat16 [2048], replicated, may hold values from -0.125 to 0.125
- expert_ids: int32 [16384, 4], P('ep'), may hold values from 0 to 59, all different within a row; in each aligned block of 256 rows (0 to 255, 256 to 511, ...) at most 32 rows name the same one
- w_gate: bfloat16 [64, 2048, 1408], P('ep', None, 'tp'), may hold values from -0.125 to 0.125
- w_up: bfloat16 [64, 2048, 1408], P('ep', None, 'tp'), may hold values from -0.125 to 0.125
- w_down: bfloat16 [64, 1408, 2048], P('ep', 'tp'), may hold values from -1.5 to 1.5
- shared_w_gate: bfloat16 [2048, 2816], P(None, 'tp'), may hold values from -0.125 to 0.125
- shared_w_up: bfloat16 [2048, 2816], P(None, 'tp'), may hold values from -0.125 to 0.125
- shared_w_down: bfloat16 [2816, 2048], P('tp'), may hold values from -0.109375 to 0.109375
Outputs:
- moe_out: bfloat16 [16384, 2048], P('ep', 'tp')
Inputs may be any that keep to these rules, and one draw needn't show every extreme that they name: `expert_ids`: each row names 4 different experts below 60. Within the 256 rows of one index of ep no expert is named by more than 32 rows, and in some of these blocks one expert is named by exactly 32 rows.
All inputs are finite; a program needn't handle non-finite values.
Results may differ from a plain program's by a relative error of at most 0.0069.
Values may be sent and summed in bfloat16 or wider, within the bound.
No kernel may reach another device: no remote copies, remote signals or barrier semaphores. Data moves between devices by JAX's collectives and lax.ppermute only.
A program may use at most 128 MiB of HBM per device.

v0:
```python
import jax
import jax.numpy as jnp
from jax import lax
from jax.sharding import PartitionSpec as P


def laid_out(parts, dim):
    lengths = list(parts.shape[1:])
    lengths[dim] *= parts.shape[0]
    return jnp.moveaxis(parts, 0, dim).reshape(lengths)


def copy_for_each(value, axis):
    peers = lax.axis_size(axis)
    return lax.all_to_all(
        jnp.broadcast_to(value[None], (peers, *value.shape)), axis, 0, 0, tiled=True
    )


def collect(value, axis, dim):
    return laid_out(copy_for_each(value, axis), dim)


def taken_together(value, axis):
    return copy_for_each(value, axis).sum(axis=0)


def turned_gather(arrays, axis, dims):
    turned = [jnp.moveaxis(a, dim, 0) for a, dim in zip(arrays, dims)]
    both = jnp.concatenate([t.reshape(len(t), -1) for t in turned], axis=1)
    out, at, done = (lax.all_gather(both, axis, axis=0, tiled=True), 0, [])
    for t, dim in zip(turned, dims):
        piece = out[:, at : at + t[0].size].reshape(-1, *t.shape[1:])
        done.append(jnp.moveaxis(piece, 0, dim))
        at += t[0].size
    return tuple(done)


def cut_along(value, dim, peers):
    before, after = (value.shape[:dim], value.shape[dim + 1 :])
    return jnp.moveaxis(value.reshape(*before, peers, -1, *after), dim, 0)


def sent_and_summed(value, axis, dim):
    peers = lax.axis_size(axis)
    parts = lax.all_to_all(cut_along(value, dim, peers), axis, 0, 0, tiled=True)
    return jnp.sum(parts.astype(jnp.float32), axis=0)


def send_back(summed):
    return lax.all_to_all(summed, "ep", split_axis=0, concat_axis=0, tiled=True)


def expert_rows(arrived, w_gate, w_up, w_down):
    share = arrived.shape[0] // lax.axis_size("tp")
    mine = lax.dynamic_slice_in_dim(arrived, lax.axis_index("tp") * share, share, 0)
    gate_act = jnp.einsum("sekd,edf->sekf", mine, w_gate, preferred_element_type=jnp.float32)
    up_act = jnp.einsum("sekd,edf->sekf", mine, w_up, preferred_element_type=jnp.float32)
    hidden = (jax.nn.silu(gate_act) * up_act).astype(jnp.bfloat16)
    full_out = jnp.einsum(
        "sekf,efd->sekd", hidden, w_down, preferred_element_type=jnp.float32
    ).astype(jnp.bfloat16)
    summed = lax.all_to_all(full_out, "tp", split_axis=3, concat_axis=0, tiled=True)
    return send_back(summed)


def per_device(
    tokens,
    norm_gain,
    router_weight,
    shared_gate_w,
    expert_ids,
    w_gate,
    w_up,
    w_down,
    shared_w_gate,
    shared_w_up,
    shared_w_down,
):
    width = tokens.shape[1]
    tok_rows = tokens.shape[0]
    column_start = lax.axis_index("tp") * width
    whole = collect(tokens, "tp", 1)
    values = whole.astype(jnp.float32)
    inv_rms = lax.rsqrt(jnp.mean(values * values, axis=-1, keepdims=True) + 1e-06)
    normed = (values * inv_rms * norm_gain[None, :]).astype(jnp.bfloat16)
    own_part = lax.dynamic_slice_in_dim(normed, column_start, width, 1)
    partial_logits = jnp.dot(own_part, router_weight, preferred_element_type=jnp.float32)
    logits = taken_together(partial_logits, "tp")
    probs = jax.nn.softmax(logits, axis=-1)
    expert_count = logits.shape[1]
    matches = expert_ids[:, :, None] == jnp.arange(expert_count, dtype=jnp.int32)[None, None, :]
    route_weight = jnp.sum(jnp.where(matches, probs[:, None, :], 0.0), axis=-1)
    gate_whole, up_whole = turned_gather((w_gate, w_up), "tp", (2, 2))
    down_whole = lax.all_gather(w_down, "tp", axis=1, tiled=True)
    experts_here = w_gate.shape[0]
    slot_count = lax.axis_size("ep") * experts_here
    capacity = tok_rows // 8
    flat_ids = expert_ids.reshape(-1)
    one_hot = (flat_ids[:, None] == jnp.arange(slot_count, dtype=jnp.int32)[None, :]).astype(
        jnp.int32
    )
    before = jnp.cumsum(one_hot, axis=0) - one_hot
    order_rank = jnp.sum(before * one_hot, axis=1)
    slot_ids = (flat_ids * capacity + order_rank).reshape(expert_ids.shape)
    targets = jnp.arange(slot_count * capacity, dtype=jnp.int32)
    dispatch_map = jnp.sum(
        (slot_ids[None, :, :] == targets[:, None, None]).astype(jnp.bfloat16), axis=2
    )
    outgoing = jnp.dot(dispatch_map, normed, preferred_element_type=jnp.float32).astype(
        jnp.bfloat16
    )
    outgoing = outgoing.reshape(lax.axis_size("ep"), experts_here, capacity, normed.shape[1])
    returned = expert_rows(
        lax.all_to_all(outgoing, "ep", split_axis=0, concat_axis=0, tiled=True),
        w_gate=gate_whole,
        w_up=up_whole,
        w_down=down_whole,
    )
    picked = returned.reshape(slot_count * capacity, width)[slot_ids]
    routed = jnp.sum(route_weight[:, :, None] * picked.astype(jnp.float32), axis=1)
    shared_gate_act = jnp.dot(normed, shared_w_gate, preferred_element_type=jnp.float32)
    shared_up_act = jnp.dot(normed, shared_w_up, preferred_element_type=jnp.float32)
    shared_hidden = (jax.nn.silu(shared_gate_act) * shared_up_act).astype(jnp.bfloat16)
    shared_part = jnp.dot(shared_hidden, shared_w_down, preferred_element_type=jnp.float32)
    shared_own = sent_and_summed(shared_part.astype(jnp.bfloat16), "tp", 1)
    share_gate = jax.nn.sigmoid(jnp.dot(normed, shared_gate_w, preferred_element_type=jnp.float32))
    return (share_gate[:, None] * shared_own + routed).astype(jnp.bfloat16)


def solution(mesh):
    return jax.shard_map(
        per_device,
        mesh=mesh,
        in_specs=(
            P("ep", "tp"),
            P(),
            P("tp", None),
            P(),
            P("ep", None),
            P("ep", None, "tp"),
            P("ep", None, "tp"),
            P("ep", "tp", None),
            P(None, "tp"),
            P(None, "tp"),
            P("tp", None),
        ),
        out_specs=P("ep", "tp"),
        check_vma=False,
    )
```

profile of v0, /device:TPU:8, one launch (start us, length us, event | category | flops | bytes accessed | tf_op | source)
XLA Modules:
  0.0 429.5 jit_solution(3899483268526843282)
XLA Ops:
  6.5 0.0 copy-start
  6.5 0.0 all-gather.3.cloned.1.call-start
  6.5 3.8 pad_maximum_fusion
  10.4 0.0 all-gather.3.cloned.1.call-update
  10.4 0.9 copy-done.3
  11.3 0.1 copy.93
  11.4 1.0 broadcast_in_dim.14
  12.5 6.4 %all-to-all-start = ((bf16[4,256,512]{1,2,0:T(8,128)(2,1)}), bf16[4,256,512]{1,2,0:T(8,128)(2,1)}, u32[]{:S(2)}, u32[]{:S(2)}) async-start(bf16[4,256,512]{1,2,0:T(8,128)(2,1)} %broadcast_in_dim.14), calls=%async_computation | async-start | bytes 2097152 | tf_op jit(solution)/shard_map/all_to_all | solution.py:15
  18.8 0.0 copy-done.5
  18.8 0.1 copy.97
  19.0 0.1 eq.58
  19.1 0.1 eq.54
  19.2 18.0 %reduce-window.6 = s32[64,8,128]{2,1,0:T(8,128)S(1)} reduce-window(s32[64,8,128]{2,1,0:T(8,128)S(1)} %fusion.47, s32[]{:T(128)} %constant.8.clone.1), window={size=1x1x128 pad=0_0x0_0x127_0}, to_apply=%region_6.7 | reduce-window | flops 8323072 | bytes 524292 | tf_op jit(solution)/shard_map/reduce-window
  37.3 0.1 slice.19
  37.4 0.1 copy.99
  37.6 0.1 copy.100
  37.7 0.1 broadcast_add_fusion
  37.8 0.1 fusion.44
  37.9 0.1 reduce_sum.83
  38.0 0.1 copy.101
  38.1 2.5 fusion.7
  40.6 0.0 all-to-all-done
  40.7 1.6 multiply_reduce_fusion.1
  42.3 1.6 fusion.32
  43.9 5.8 %convolution_convert_fusion = bf16[2048,2048]{1,0:T(8,128)(2,1)} fusion(bf16[2048,256]{1,0:T(8,128)(2,1)S(1)} %copy-done.2, bf16[256,2048]{0,1:T(8,128)(2,1)S(1)} %fusion.32), kind=kOutput, calls=%fused_computation.3 | convolution fusion | flops 2151677952 | bytes 10485760 | tf_op jit(solution)/shard_map/dot_general | solution.py:110
  49.7 0.0 copy-done.1
  49.7 10.9 %all-to-all-start.3 = ((bf16[64,1,32,2048]{3,2,1,0:T(8,128)(2,1)}), bf16[64,1,32,2048]{3,2,1,0:T(8,128)(2,1)}, u32[]{:S(2)}, u32[]{:S(2)}) async-start(bf16[64,1,32,2048]{3,2,1,0:T(8,128)(2,1)} %bitcast.131), calls=%async_computation.3 | async-start | bytes 16777216 | tf_op jit(solution)/shard_map/all_to_all | solution.py:115
  60.6 0.0 all-gather.5.cloned.1.call-start
  60.6 0.7 all-gather.5.cloned.1.call-update
  61.4 1.1 fusion.45
  62.5 63.2 %all-gather.3.cloned.1.call-done = bf16[1408,4096]{1,0:T(8,128)(2,1)} async-done(((bf16[352,4096]{1,0:T(8,128)(2,1)}), bf16[1408,4096]{1,0:T(8,128)(2,1)}) %all-gather.3.cloned.1.call-update) | async-done | bytes 11534352 | tf_op jit(solution)/shard_map/all_gather | solution.py:31
  125.7 11.0 %fusion.56 = (bf16[1408,2048]{1,0:T(8,128)(2,1)}, bf16[1408,2048]{1,0:T(8,128)(2,1)}) fusion(bf16[1408,4096]{1,0:T(8,128)(2,1)} %all-gather.3.cloned.1.call-done), kind=kLoop, calls=%fused_computation.61 | loop fusion | bytes 23068672 | tf_op jit(solution)/shard_map/slice | solution.py:33
  136.6 8.5 %copy.110 = bf16[1408,2048]{0,1:T(8,128)(2,1)} copy(bf16[1408,2048]{1,0:T(8,128)(2,1)} %get-tuple-element.7) | data formatting | bytes 11534336
  145.2 8.4 %copy.111 = bf16[1408,2048]{0,1:T(8,128)(2,1)} copy(bf16[1408,2048]{1,0:T(8,128)(2,1)} %get-tuple-element.8) | data formatting | bytes 11534336
  153.5 93.2 %all-to-all-done.3 = bf16[64,1,32,2048]{3,2,1,0:T(8,128)(2,1)} async-done(((bf16[64,1,32,2048]{3,2,1,0:T(8,128)(2,1)}), bf16[64,1,32,2048]{3,2,1,0:T(8,128)(2,1)}, u32[]{:S(2)}, u32[]{:S(2)}) %all-to-all-start.3) | async-done | bytes 8388640 | tf_op jit(solution)/shard_map/all_to_all | solution.py:115
  246.8 0.7 broadcast_in_dim.15
  247.5 4.8 %all-to-all-start.2 = ((f32[4,256,60]{1,2,0:T(8,128)}), f32[4,256,60]{1,2,0:T(8,128)S(1)}, u32[]{:S(2)}, u32[]{:S(2)}) async-start(f32[4,256,60]{1,2,0:T(8,128)} %broadcast_in_dim.15), calls=%async_computation.2 | async-start | bytes 524288 | tf_op jit(solution)/shard_map/all_to_all | solution.py:15
  252.3 8.3 %fusion.8 = f32[16,1,32,1408]{3,2,0,1:T(8,128)} fusion(bf16[1408,2048]{0,1:T(8,128)(2,1)} %copy.110, bf16[64,1,32,2048]{3,2,1,0:T(8,128)(2,1)} %all-to-all-done.3, s32[]{:T(128)S(6)} %select_n.15), kind=kOutput, calls=%fused_computation.11 | convolution fusion | flops 2952790016 | bytes 10747908 | tf_op jit(solution)/shard_map/sekd,edf->sekf/dot_general | solution.py:57
  260.6 14.2 %fusion.23 = bf16[16,1,32,2048]{3,2,0,1:T(8,128)(2,1)} fusion(bf16[1,1408,2048]{2,1,0:T(8,128)(2,1)} %all-gather.5.cloned.1.call-done, bf16[1408,2048]{0,1:T(8,128)(2,1)} %copy.111, f32[16,1,32,1408]{3,2,0,1:T(8,128)} %fusion.8, bf16[64,1,32,2048]{3,2,1,0:T(8,128)(2,1)} %all-to-all-done.3, s32[]{:T(128)S(6)} %select_n.15), kind=kOutput, calls=%fused_computation.17 | convolution fusion | flops 5910953984 | bytes 18612228 | tf_op jit(solution)/shard_map/sekf,efd->sekd/dot_general | solution.py:60
  274.8 9.9 %copy.104 = bf16[16,1,32,2048]{2,0,1,3:T(8,128)(2,1)} copy(bf16[16,1,32,2048]{3,2,0,1:T(8,128)(2,1)} %fusion.23) | data formatting | bytes 4194304 | tf_op jit(solution)/shard_map/convert_element_type | solution.py:62
  284.7 10.6 %reshape.141 = bf16[4,2,131072]{2,1,0:T(2,128)(2,1)} reshape(bf16[2048,1,16,32]{3,2,1,0:T(8,128)(2,1)} %bitcast.132) | data formatting | bytes 4194304
  295.3 0.0 all-to-all-done.2
  295.3 4.8 %all-to-all-start.4 = ((bf16[4,2,131072]{2,1,0:T(2,128)(2,1)}), bf16[4,2,131072]{2,1,0:T(2,128)(2,1)}, u32[]{:S(2)}, u32[]{:S(2)}) async-start(bf16[4,2,131072]{2,1,0:T(2,128)(2,1)} %reshape.141), calls=%async_computation.4 | async-start | bytes 4194304 | tf_op jit(solution)/shard_map/all_to_all | solution.py:63
  300.1 3.9 fusion.58
  304.0 6.5 %convolution_convert_fusion.1 = bf16[256,2048]{1,0:T(8,128)(2,1)} fusion(bf16[704,2048]{1,0:T(8,128)(2,1)S(1)} %copy-done, bf16[2048,704]{0,1:T(8,128)(2,1)} %param.20, bf16[256,2048]{0,1:T(8,128)(2,1)} %copy-done.1, f32[256,704]{0,1:T(8,128)} %fusion.58), kind=kOutput, calls=%fused_computation.19 | convolution fusion | flops 1478000640 | bytes 8585216 | tf_op jit(solution)/shard_map/dot_general | solution.py:125
  310.5 2.4 copy.116
  312.9 8.3 %all-to-all-done.4 = bf16[4,2,131072]{2,1,0:T(2,128)(2,1)} async-done(((bf16[4,2,131072]{2,1,0:T(2,128)(2,1)}), bf16[4,2,131072]{2,1,0:T(2,128)(2,1)}, u32[]{:S(2)}, u32[]{:S(2)}) %all-to-all-start.4) | async-done | bytes 2097184 | tf_op jit(solution)/shard_map/all_to_all | solution.py:63
  321.1 5.7 %all-to-all-start.1 = ((bf16[4,256,512]{2,1,0:T(8,128)(2,1)}), bf16[4,256,512]{2,1,0:T(8,128)(2,1)}, u32[]{:S(2)}, u32[]{:S(2)}) async-start(bf16[4,256,512]{2,1,0:T(8,128)(2,1)} %bitcast.136), calls=%async_computation.1 | async-start | bytes 2097152 | tf_op jit(solution)/shard_map/all_to_all | solution.py:46
  326.8 7.4 %reshape.142 = bf16[2048,1,16,32]{3,2,1,0:T(8,128)(2,1)} reshape(bf16[4,2,131072]{2,1,0:T(2,128)(2,1)} %all-to-all-done.4) | data formatting | bytes 4194304
  334.2 9.9 %copy.109 = bf16[16,1,32,4,512]{4,3,2,0,1:T(4,128)(2,1)} copy(bf16[16,1,32,4,512]{2,0,4,3,1:T(8,128)(2,1)} %bitcast.133) | data formatting | bytes 4194304 | tf_op jit(solution)/shard_map/all_to_all | solution.py:63
  344.1 3.4 copy.106
  347.6 0.0 all-to-all-done.1
  347.6 10.4 %all-to-all-start.5 = ((bf16[64,1,32,512]{3,2,1,0:T(8,128)(2,1)}), bf16[64,1,32,512]{3,2,1,0:T(8,128)(2,1)}, u32[]{:S(2)}, u32[]{:S(2)}) async-start(bf16[64,1,32,512]{3,2,1,0:T(8,128)(2,1)} %bitcast.135), calls=%async_computation.5 | async-start | bytes 4194304 | tf_op jit(solution)/shard_map/all_to_all | solution.py:51
  358.0 0.1 copy.108
  358.1 0.1 reshape.127
  358.3 1.5 fusion.57
  359.9 0.1 select_reduce_fusion
  360.0 0.1 copy.95
  360.1 1.5 convert_reduce_fusion
  361.6 47.6 %all-to-all-done.5 = bf16[64,1,32,512]{3,2,1,0:T(8,128)(2,1)} async-done(((bf16[64,1,32,512]{3,2,1,0:T(8,128)(2,1)}), bf16[64,1,32,512]{3,2,1,0:T(8,128)(2,1)}, u32[]{:S(2)}, u32[]{:S(2)}) %all-to-all-start.5) | async-done | bytes 2097184 | tf_op jit(solution)/shard_map/all_to_all | solution.py:51
  409.1 7.0 %gather_fusion = bf16[1024,512]{1,0:T(8,128)(2,1)} fusion(bf16[2048,512]{1,0:T(8,128)(2,1)} %bitcast.36, s32[1024]{0:T(1024)S(1)} %broadcast_clamp_fusion), kind=kCustom, calls=%fused_computation | custom fusion | bytes 2101248 | tf_op jit(solution)/shard_map/gather | solution.py:120
  416.1 2.8 reshape.135
  418.8 3.0 multiply_reduce_fusion
  421.8 0.8 add_convert_fusion
  (25 shorter events, 0.2 us)
Async XLA Ops:
  6.5 297.4 %copy-start = (bf16[704,2048]{1,0:T(8,128)(2,1)S(1)}, bf16[704,2048]{1,0:T(8,128)(2,1)}, u32[]{:S(2)}) copy-start(bf16[704,2048]{1,0:T(8,128)(2,1)} %param.21) | copy-start | bytes 8650756
  6.5 119.1 %all-gather.3.cloned.1.call-start = ((), (), s32[]{:S(2)}) async-start(), calls=%async_computation.6 | async-start | bytes 14417920 | tf_op jit(solution)/shard_map/all_gather | solution.py:31
  10.3 0.9 copy-start.3
  10.4 8.5 %copy-start.5 = (s32[256,4]{0,1:T(4,128)S(1)}, s32[256,4]{0,1:T(4,128)}, u32[]{:S(2)}) copy-start(s32[256,4]{0,1:T(4,128)} %param.15) | copy-start | bytes 12292
  12.5 28.2 %all-to-all-start = ((bf16[4,256,512]{1,2,0:T(8,128)(2,1)}), bf16[4,256,512]{1,2,0:T(8,128)(2,1)}, u32[]{:S(2)}, u32[]{:S(2)}) async-start(bf16[4,256,512]{1,2,0:T(8,128)(2,1)} %broadcast_in_dim.14), calls=%async_computation | async-start | bytes 2097152 | tf_op jit(solution)/shard_map/all_to_all | solution.py:15
  18.8 23.5 %copy-start.6 = (f32[2048]{0:T(1024)S(1)}, f32[2048]{0:T(1024)}, u32[]{:S(2)}) copy-start(f32[2048]{0:T(1024)} %param.12) | copy-start | bytes 24580
  40.7 3.2 copy-start.2
  43.9 5.8 %copy-start.1 = (bf16[256,2048]{0,1:T(8,128)(2,1)}, bf16[256,2048]{0,1:T(8,128)(2,1)S(1)}, u32[]{:S(2)}) copy-start(bf16[256,2048]{0,1:T(8,128)(2,1)S(1)} %fusion.32) | copy-start | bytes 3145732
  49.7 11.7 %copy-start.4 = (bf16[512,60]{0,1:T(8,128)(2,1)S(1)}, bf16[512,60]{0,1:T(8,128)(2,1)}, u32[]{:S(2)}) copy-start(bf16[512,60]{0,1:T(8,128)(2,1)} %param.13) | copy-start | bytes 184324
  49.7 197.1 %all-to-all-start.3 = ((bf16[64,1,32,2048]{3,2,1,0:T(8,128)(2,1)}), bf16[64,1,32,2048]{3,2,1,0:T(8,128)(2,1)}, u32[]{:S(2)}, u32[]{:S(2)}) async-start(bf16[64,1,32,2048]{3,2,1,0:T(8,128)(2,1)} %bitcast.131), calls=%async_computation.3 | async-start | bytes 16777216 | tf_op jit(solution)/shard_map/all_to_all | solution.py:115
  60.6 200.0 %all-gather.5.cloned.1.call-start = ((), (), s32[]{:S(2)}) async-start(), calls=%async_computation.7 | async-start | bytes 7208960 | tf_op jit(solution)/shard_map/all_gather | solution.py:95
  247.5 47.8 %all-to-all-start.2 = ((f32[4,256,60]{1,2,0:T(8,128)}), f32[4,256,60]{1,2,0:T(8,128)S(1)}, u32[]{:S(2)}, u32[]{:S(2)}) async-start(f32[4,256,60]{1,2,0:T(8,128)} %broadcast_in_dim.15), calls=%async_computation.2 | async-start | bytes 524288 | tf_op jit(solution)/shard_map/all_to_all | solution.py:15
  295.3 25.9 %all-to-all-start.4 = ((bf16[4,2,131072]{2,1,0:T(2,128)(2,1)}), bf16[4,2,131072]{2,1,0:T(2,128)(2,1)}, u32[]{:S(2)}, u32[]{:S(2)}) async-start(bf16[4,2,131072]{2,1,0:T(2,128)(2,1)} %reshape.141), calls=%async_computation.4 | async-start | bytes 4194304 | tf_op jit(solution)/shard_map/all_to_all | solution.py:63
  321.1 26.4 %all-to-all-start.1 = ((bf16[4,256,512]{2,1,0:T(8,128)(2,1)}), bf16[4,256,512]{2,1,0:T(8,128)(2,1)}, u32[]{:S(2)}, u32[]{:S(2)}) async-start(bf16[4,256,512]{2,1,0:T(8,128)(2,1)} %bitcast.136), calls=%async_computation.1 | async-start | bytes 2097152 | tf_op jit(solution)/shard_map/all_to_all | solution.py:46
  347.6 10.6 %copy-start.7 = (bf16[2048]{0:T(1024)(128)(2,1)S(1)}, bf16[2048]{0:T(1024)(128)(2,1)}, u32[]{:S(2)}) copy-start(bf16[2048]{0:T(1024)(128)(2,1)} %param.14) | copy-start | bytes 12292
  347.6 61.6 %all-to-all-start.5 = ((bf16[64,1,32,512]{3,2,1,0:T(8,128)(2,1)}), bf16[64,1,32,512]{3,2,1,0:T(8,128)(2,1)}, u32[]{:S(2)}, u32[]{:S(2)}) async-start(bf16[64,1,32,512]{3,2,1,0:T(8,128)(2,1)} %bitcast.135), calls=%async_computation.5 | async-start | bytes 4194304 | tf_op jit(solution)/shard_map/all_to_all | solution.py:51
Sparse Core Ops, SparseCore 0:
  10.5 115.1 all-gather.2
  127.5 64.4 all-gather.4
where the time goes:
time: 431 us; the launch traced here: 429 us
  waiting for transfers between devices  213 us (49%)
  local copies, waits for them, and re-layouts  85.4 us (20%)
  starting transfers between devices  42.9 us (10%)
  matrix products  41.3 us (10%)
  other arithmetic  33.3 us (8%)
  between operations  13.6 us (3%)
    all_to_all x1, waiting for transfers between devices, per_device(): lax.all_to_all(outgoing, 'ep', split_axis=0, concat_axis=0, tiled=True)  93.2 us
    all_gather x1, waiting for transfers between devices, turned_gather(): out, at, done = (lax.all_gather(both, axis, axis=0, tiled=True), 0, [])  63.2 us
    all_to_all x1, waiting for transfers between devices, send_back(): return lax.all_to_all(summed, 'ep', split_axis=0, concat_axis=0, tiled=True)  47.6 us
    unnamed x23, local copies, waits for them, and re-layouts  36.1 us
    another operation x3, other arithmetic  18.2 us
    dot_general x1, matrix products, expert_rows(): jnp.einsum('sekf,efd->sekd', hidden, w_down, preferred_element_type=jnp.f...  14.2 us
    all_to_all x2, local copies, waits for them, and re-layouts, expert_rows(): lax.all_to_all(full_out, 'tp', split_axis=3, concat_axis=0, tiled=True)  13.4 us
    all_to_all x2, starting transfers between devices, copy_for_each(): lax.all_to_all(jnp.broadcast_to(value[None], (peers, *value.shape)), axis...  11.2 us
  transfers between devices with their start and end apart: 8, of which 4 were waited for; matrix products, arithmetic and copies ran while one was open for 33% of the time, Pallas kernels for 0%

commit v1 on v0

--- a/solution.py
+++ b/solution.py
@@ -2,6 +2,28 @@
 import jax.numpy as jnp
 from jax import lax
 from jax.sharding import PartitionSpec as P
+
+
+def split_up(x, dim, length):
+    before, after = (x.shape[:dim], x.shape[dim + 1 :])
+    return jnp.moveaxis(x.reshape(*before, length, -1, *after), dim, 0)
+
+
+def joined_along(blocks, dim):
+    shape = list(blocks.shape[1:])
+    shape[dim] *= blocks.shape[0]
+    return jnp.moveaxis(blocks, 0, dim).reshape(shape)
+
+
+def exchange_directly(shard, axis, split_dim, concat_dim):
+    size, position = (lax.axis_size(axis), lax.axis_index(axis))
+    pieces = split_up(shard, split_dim, size)
+    gathered = [pieces[position]]
+    for hop in range(1, size):
+        sent = pieces[(position + hop) % size]
+        gathered.append(lax.ppermute(sent, axis, [(i, (i + hop) % size) for i in range(size)]))
+    pieces = jnp.stack(gathered)[(position - jnp.arange(size)) % size]
+    return joined_along(pieces, concat_dim)
 
 
 def laid_out(parts, dim):
@@ -60,7 +82,7 @@
     full_out = jnp.einsum(
         "sekf,efd->sekd", hidden, w_down, preferred_element_type=jnp.float32
     ).astype(jnp.bfloat16)
-    summed = lax.all_to_all(full_out, "tp", split_axis=3, concat_axis=0, tiled=True)
+    summed = exchange_directly(full_out, "tp", 3, 0)
     return send_back(summed)
 
 

time: 431 us -> 401 us (0.930)
  local copies, waits for them, and re-layouts: 85.4 us -> 54.5 us
    ppermute x0 -> x3, waiting for transfers between devices: none -> 21.6 us  [exchange_directly(): lax.ppermute(sent, axis, [(i, (i + hop) % size) for i in range(size)])]
    unnamed x23 -> x29, local copies, waits for them, and re-layouts: 36.1 us -> 18.6 us
    all_to_all x2 -> x0, local copies, waits for them, and re-layouts: 13.4 us -> none  [expert_rows(): lax.all_to_all(full_out, 'tp', split_axis=3, concat_axis=0, tiled=True)]
    all_gather x1, waiting for transfers between devices: 63.2 us -> 50.4 us  [turned_gather(): out, at, done = (lax.all_gather(both, axis, axis=0, tiled=True), 0, [])]
    convert_element_type x1 -> x0, local copies, waits for them, and re-layouts: 9.95 us -> none  [expert_rows(): full_out = jnp.einsum('sekf,efd->sekd', hidden, w_down, preferred_element...]
    all_to_all x1 -> x0, waiting for transfers between devices: 8.27 us -> none  [expert_rows(): lax.all_to_all(full_out, 'tp', split_axis=3, concat_axis=0, tiled=True)]
    ppermute x0 -> x3, starting transfers between devices: none -> 5.2 us  [exchange_directly(): lax.ppermute(sent, axis, [(i, (i + hop) % size) for i in range(size)])]
    all_to_all x1 -> x0, starting transfers between devices: 4.8 us -> none  [expert_rows(): lax.all_to_all(full_out, 'tp', split_axis=3, concat_axis=0, tiled=True)]
  transfers between devices with their start and end apart: 8 -> 10, of which waited for: 4 -> 5; matrix products, arithmetic and copies ran while one was open for 33% -> 28% of each run, Pallas kernels for 0% -> 0%
where the time goes in v1:
time: 401 us; the launch traced here: 399 us
  waiting for transfers between devices  214 us (53%)
  local copies, waits for them, and re-layouts  54.5 us (14%)
  starting transfers between devices  42.4 us (11%)
  matrix products  40.1 us (10%)
  other arithmetic  33.6 us (8%)
  between operations  13.7 us (3%)
    all_to_all x1, waiting for transfers between devices, per_device(): lax.all_to_all(outgoing, 'ep', split_axis=0, concat_axis=0, tiled=True)  93.1 us
    all_gather x1, waiting for transfers between devices, turned_gather(): out, at, done = (lax.all_gather(both, axis, axis=0, tiled=True), 0, [])  50.4 us
    all_to_all x1, waiting for transfers between devices, send_back(): return lax.all_to_all(summed, 'ep', split_axis=0, concat_axis=0, tiled=True)  48.8 us
    ppermute x3, waiting for transfers between devices, exchange_directly(): lax.ppermute(sent, axis, [(i, (i + hop) % size) for i in range(size)])  21.6 us
    unnamed x29, local copies, waits for them, and re-layouts  18.6 us
    another operation x3, other arithmetic  18.2 us
    dot_general x1, matrix products, expert_rows(): jnp.einsum('sekf,efd->sekd', hidden, w_down, preferred_element_type=jnp.f...  14.1 us
    all_to_all x2, starting transfers between devices, copy_for_each(): lax.all_to_all(jnp.broadcast_to(value[None], (peers, *value.shape)), axis...  11.2 us
  transfers between devices with their start and end apart: 10, of which 5 were waited for; matrix products, arithmetic and copies ran while one was open for 28% of the time, Pallas kernels for 0%

profile of v1, /device:TPU:8, one launch (start us, length us, event | category | flops | bytes accessed | tf_op | source)
XLA Modules:
  0.0 398.7 jit_solution(4577122277651311465)
XLA Ops:
  6.5 3.8 pad_maximum_fusion
  10.4 0.0 all-gather.3.cloned.1.call-update
  10.4 0.9 copy-done.5
  11.3 0.1 copy.85
  11.4 1.0 broadcast_in_dim.14
  12.5 6.4 %all-to-all-start = ((bf16[4,256,512]{1,2,0:T(8,128)(2,1)}), bf16[4,256,512]{1,2,0:T(8,128)(2,1)}, u32[]{:S(2)}, u32[]{:S(2)}) async-start(bf16[4,256,512]{1,2,0:T(8,128)(2,1)} %broadcast_in_dim.14), calls=%async_computation | async-start | bytes 2097152 | tf_op jit(solution)/shard_map/all_to_all | solution.py:37
  18.8 0.1 copy.89
  19.0 0.1 eq.64
  19.1 0.1 eq.60
  19.2 18.0 %reduce-window.6 = s32[64,8,128]{2,1,0:T(8,128)S(1)} reduce-window(s32[64,8,128]{2,1,0:T(8,128)S(1)} %fusion.47, s32[]{:T(128)} %constant.62.clone.1), window={size=1x1x128 pad=0_0x0_0x127_0}, to_apply=%region_6.7 | reduce-window | flops 8323072 | bytes 524292 | tf_op jit(solution)/shard_map/reduce-window
  37.3 0.1 slice.21
  37.4 0.1 copy.91
  37.6 0.1 copy.92
  37.7 0.1 broadcast_add_fusion
  37.8 0.1 fusion.44
  37.9 0.1 reduce_sum.83
  38.0 0.1 copy.93
  38.1 2.5 fusion.7
  40.7 1.6 multiply_reduce_fusion.1
  42.3 1.6 fusion.32
  43.9 5.8 %convolution_convert_fusion = bf16[2048,2048]{1,0:T(8,128)(2,1)} fusion(bf16[2048,256]{1,0:T(8,128)(2,1)S(1)} %copy-done.4, bf16[256,2048]{0,1:T(8,128)(2,1)S(1)} %fusion.32), kind=kOutput, calls=%fused_computation.4 | convolution fusion | flops 2151677952 | bytes 10485760 | tf_op jit(solution)/shard_map/dot_general | solution.py:132
  49.7 10.8 %all-to-all-start.3 = ((bf16[64,1,32,2048]{3,2,1,0:T(8,128)(2,1)}), bf16[64,1,32,2048]{3,2,1,0:T(8,128)(2,1)}, u32[]{:S(2)}, u32[]{:S(2)}) async-start(bf16[64,1,32,2048]{3,2,1,0:T(8,128)(2,1)} %bitcast.150), calls=%async_computation.3 | async-start | bytes 16777216 | tf_op jit(solution)/shard_map/all_to_all | solution.py:137
  60.5 0.2 all-gather.5.cloned.1.call-start
  60.7 0.5 all-gather.5.cloned.1.call-update
  61.3 3.9 fusion.60
  65.1 6.7 %convolution_convert_fusion.1 = bf16[256,2048]{1,0:T(8,128)(2,1)} fusion(bf16[704,2048]{1,0:T(8,128)(2,1)S(1)} %copy-done, bf16[2048,704]{0,1:T(8,128)(2,1)} %param.20, bf16[256,2048]{0,1:T(8,128)(2,1)} %copy-done.2, f32[256,704]{0,1:T(8,128)} %fusion.60), kind=kOutput, calls=%fused_computation.20 | convolution fusion | flops 1478000640 | bytes 8585216 | tf_op jit(solution)/shard_map/dot_general | solution.py:147
  71.8 2.3 copy.116
  74.1 1.1 fusion.45
  75.3 50.4 %all-gather.3.cloned.1.call-done = bf16[1408,4096]{1,0:T(8,128)(2,1)} async-done(((bf16[352,4096]{1,0:T(8,128)(2,1)}), bf16[1408,4096]{1,0:T(8,128)(2,1)}) %all-gather.3.cloned.1.call-update) | async-done | bytes 11534352 | tf_op jit(solution)/shard_map/all_gather | solution.py:53
  125.7 11.0 %fusion.58 = (bf16[1408,2048]{1,0:T(8,128)(2,1)}, bf16[1408,2048]{1,0:T(8,128)(2,1)}) fusion(bf16[1408,4096]{1,0:T(8,128)(2,1)} %all-gather.3.cloned.1.call-done), kind=kLoop, calls=%fused_computation.78 | loop fusion | bytes 23068672 | tf_op jit(solution)/shard_map/slice | solution.py:55
  136.6 8.5 %copy.102 = bf16[1408,2048]{0,1:T(8,128)(2,1)} copy(bf16[1408,2048]{1,0:T(8,128)(2,1)} %get-tuple-element.7) | data formatting | bytes 11534336
  145.2 8.4 %copy.103 = bf16[1408,2048]{0,1:T(8,128)(2,1)} copy(bf16[1408,2048]{1,0:T(8,128)(2,1)} %get-tuple-element.8) | data formatting | bytes 11534336
  153.5 93.1 %all-to-all-done.3 = bf16[64,1,32,2048]{3,2,1,0:T(8,128)(2,1)} async-done(((bf16[64,1,32,2048]{3,2,1,0:T(8,128)(2,1)}), bf16[64,1,32,2048]{3,2,1,0:T(8,128)(2,1)}, u32[]{:S(2)}, u32[]{:S(2)}) %all-to-all-start.3) | async-done | bytes 8388640 | tf_op jit(solution)/shard_map/all_to_all | solution.py:137
  246.6 0.7 broadcast_in_dim.15
  247.3 4.8 %all-to-all-start.2 = ((f32[4,256,60]{1,2,0:T(8,128)}), f32[4,256,60]{1,2,0:T(8,128)S(1)}, u32[]{:S(2)}, u32[]{:S(2)}) async-start(f32[4,256,60]{1,2,0:T(8,128)} %broadcast_in_dim.15), calls=%async_computation.2 | async-start | bytes 524288 | tf_op jit(solution)/shard_map/all_to_all | solution.py:37
  252.2 8.3 %fusion.8 = f32[16,1,32,1408]{3,2,0,1:T(8,128)} fusion(bf16[1408,2048]{0,1:T(8,128)(2,1)} %copy.102, bf16[64,1,32,2048]{3,2,1,0:T(8,128)(2,1)} %all-to-all-done.3, s32[]{:T(128)S(6)} %select_n.65), kind=kOutput, calls=%fused_computation.12 | convolution fusion | flops 2952790016 | bytes 10747908 | tf_op jit(solution)/shard_map/sekd,edf->sekf/dot_general | solution.py:79
  260.5 14.1 %fusion.23 = bf16[16,1,32,2048]{3,2,0,1:T(8,128)(2,1)} fusion(bf16[1,1408,2048]{2,1,0:T(8,128)(2,1)} %all-gather.5.cloned.1.call-done, bf16[1408,2048]{0,1:T(8,128)(2,1)} %copy.103, f32[16,1,32,1408]{3,2,0,1:T(8,128)} %fusion.8, bf16[64,1,32,2048]{3,2,1,0:T(8,128)(2,1)} %all-to-all-done.3, s32[]{:T(128)S(6)} %select_n.65), kind=kOutput, calls=%fused_computation.18 | convolution fusion | flops 5910953984 | bytes 18612228 | tf_op jit(solution)/shard_map/sekf,efd->sekd/dot_general | solution.py:82
  274.6 3.3 reshape.185
  277.9 0.0 all-to-all-done.2
  277.9 4.8 %all-to-all-start.1 = ((bf16[4,256,512]{2,1,0:T(8,128)(2,1)}), bf16[4,256,512]{2,1,0:T(8,128)(2,1)}, u32[]{:S(2)}, u32[]{:S(2)}) async-start(bf16[4,256,512]{2,1,0:T(8,128)(2,1)} %bitcast.152), calls=%async_computation.1 | async-start | bytes 2097152 | tf_op jit(solution)/shard_map/all_to_all | solution.py:68
  282.7 4.4 %constant_dynamic-slice_fusion.3 = (bf16[16,1,32,1,512]{4,3,2,0,1:T(2,128)(2,1)S(1)}, bf16[16,1,32,1,512]{4,3,2,0,1:T(2,128)(2,1)S(1)}, bf16[16,1,32,1,512]{4,3,...) fusion(bf16[16,1,32,4,512]{4,3,2,0,1:T(4,128)(2,1)S(1)} %reshape.185, s32[]{:T(128)S(6)} %select_n.66, s32[]{:T(128)S(6)} %select_n.70, ...), kind=kLoop, calls=%fused_computation.68 | loop fusion | bytes 4194320 | tf_op jit(solution)/shard_map/dynamic-slice
  287.1 0.1 copy.119
  287.3 1.5 collective-permute-start
  288.8 0.1 copy.118
  288.9 1.0 collective-permute-start.1
  289.9 0.1 copy.117
  290.1 2.7 collective-permute-start.2
  292.8 0.1 copy.120
  292.9 19.1 %collective-permute-done = bf16[16,1,32,512]{3,2,0,1:T(8,128)(2,1)S(1)} collective-permute-done((bf16[16,1,32,512]{3,2,0,1:T(8,128)(2,1)S(1)}, bf16[16,1,32,512]{3,2,0,1:T(8,128)(2,1)S(1)}, u32[]{:S(2)}, u32[]{:S(2)}) %collective-permute-start) | collective-permute-done | bytes 524320 | tf_op jit(solution)/shard_map/ppermute | solution.py:24
  312.1 2.4 collective-permute-done.2
  314.5 0.3 maximum_bitcast_fusion
  314.8 2.0 gather_fusion
  316.8 10.2 %all-to-all-start.4 = ((bf16[64,1,32,512]{3,2,1,0:T(8,128)(2,1)}), bf16[64,1,32,512]{3,2,1,0:T(8,128)(2,1)}, u32[]{:S(2)}, u32[]{:S(2)}) async-start(bf16[64,1,32,512]{3,2,1,0:T(8,128)(2,1)} %bitcast.151), calls=%async_computation.4 | async-start | bytes 4194304 | tf_op jit(solution)/shard_map/all_to_all | solution.py:73
  327.0 0.1 copy.101
  327.1 0.1 reshape.201
  327.3 0.2 fusion.59
  327.7 0.1 select_reduce_fusion
  327.8 0.1 copy.87
  327.9 1.5 convert_reduce_fusion
  329.4 48.8 %all-to-all-done.4 = bf16[64,1,32,512]{3,2,1,0:T(8,128)(2,1)} async-done(((bf16[64,1,32,512]{3,2,1,0:T(8,128)(2,1)}), bf16[64,1,32,512]{3,2,1,0:T(8,128)(2,1)}, u32[]{:S(2)}, u32[]{:S(2)}) %all-to-all-start.4) | async-done | bytes 2097184 | tf_op jit(solution)/shard_map/all_to_all | solution.py:73
  378.2 7.1 %gather_fusion.1 = bf16[1024,512]{1,0:T(8,128)(2,1)} fusion(bf16[2048,512]{1,0:T(8,128)(2,1)} %bitcast.43, s32[1024]{0:T(1024)S(1)} %broadcast_clamp_fusion), kind=kCustom, calls=%fused_computation.1 | custom fusion | bytes 2101248 | tf_op jit(solution)/shard_map/gather | solution.py:142
  385.3 2.8 reshape.210
  388.0 3.0 multiply_reduce_fusion
  391.0 0.8 add_convert_fusion
  (38 shorter events, 0.3 us)
Async XLA Ops:
  6.5 58.6 %copy-start = (bf16[704,2048]{1,0:T(8,128)(2,1)S(1)}, bf16[704,2048]{1,0:T(8,128)(2,1)}, u32[]{:S(2)}) copy-start(bf16[704,2048]{1,0:T(8,128)(2,1)} %param.21) | copy-start | bytes 8650756
  6.5 119.1 %all-gather.3.cloned.1.call-start = ((), (), s32[]{:S(2)}) async-start(), calls=%async_computation.5 | async-start | bytes 14417920 | tf_op jit(solution)/shard_map/all_gather | solution.py:53
  10.3 0.9 copy-start.5
  10.4 8.5 %copy-start.7 = (s32[256,4]{0,1:T(4,128)S(1)}, s32[256,4]{0,1:T(4,128)}, u32[]{:S(2)}) copy-start(s32[256,4]{0,1:T(4,128)} %param.15) | copy-start | bytes 12292
  12.5 28.2 %all-to-all-start = ((bf16[4,256,512]{1,2,0:T(8,128)(2,1)}), bf16[4,256,512]{1,2,0:T(8,128)(2,1)}, u32[]{:S(2)}, u32[]{:S(2)}) async-start(bf16[4,256,512]{1,2,0:T(8,128)(2,1)} %broadcast_in_dim.14), calls=%async_computation | async-start | bytes 2097152 | tf_op jit(solution)/shard_map/all_to_all | solution.py:37
  18.8 23.5 %copy-start.8 = (f32[2048]{0:T(1024)S(1)}, f32[2048]{0:T(1024)}, u32[]{:S(2)}) copy-start(f32[2048]{0:T(1024)} %param.12) | copy-start | bytes 24580
  40.7 3.2 copy-start.4
  43.9 5.8 %copy-start.2 = (bf16[256,2048]{0,1:T(8,128)(2,1)}, bf16[256,2048]{0,1:T(8,128)(2,1)S(1)}, u32[]{:S(2)}) copy-start(bf16[256,2048]{0,1:T(8,128)(2,1)S(1)} %fusion.32) | copy-start | bytes 3145732
  49.7 196.9 %all-to-all-start.3 = ((bf16[64,1,32,2048]{3,2,1,0:T(8,128)(2,1)}), bf16[64,1,32,2048]{3,2,1,0:T(8,128)(2,1)}, u32[]{:S(2)}, u32[]{:S(2)}) async-start(bf16[64,1,32,2048]{3,2,1,0:T(8,128)(2,1)} %bitcast.150), calls=%async_computation.3 | async-start | bytes 16777216 | tf_op jit(solution)/shard_map/all_to_all | solution.py:137
  60.5 200.0 %all-gather.5.cloned.1.call-start = ((), (), s32[]{:S(2)}) async-start(), calls=%async_computation.6 | async-start | bytes 7208960 | tf_op jit(solution)/shard_map/all_gather | solution.py:117
  65.1 9.0 %copy-start.6 = (bf16[512,60]{0,1:T(8,128)(2,1)S(1)}, bf16[512,60]{0,1:T(8,128)(2,1)}, u32[]{:S(2)}) copy-start(bf16[512,60]{0,1:T(8,128)(2,1)} %param.13) | copy-start | bytes 184324
  247.3 30.5 %all-to-all-start.2 = ((f32[4,256,60]{1,2,0:T(8,128)}), f32[4,256,60]{1,2,0:T(8,128)S(1)}, u32[]{:S(2)}, u32[]{:S(2)}) async-start(f32[4,256,60]{1,2,0:T(8,128)} %broadcast_in_dim.15), calls=%async_computation.2 | async-start | bytes 524288 | tf_op jit(solution)/shard_map/all_to_all | solution.py:37
  277.9 38.9 %all-to-all-start.1 = ((bf16[4,256,512]{2,1,0:T(8,128)(2,1)}), bf16[4,256,512]{2,1,0:T(8,128)(2,1)}, u32[]{:S(2)}, u32[]{:S(2)}) async-start(bf16[4,256,512]{2,1,0:T(8,128)(2,1)} %bitcast.152), calls=%async_computation.1 | async-start | bytes 2097152 | tf_op jit(solution)/shard_map/all_to_all | solution.py:68
  287.3 24.8 %collective-permute-start = (bf16[16,1,32,512]{3,2,0,1:T(8,128)(2,1)S(1)}, bf16[16,1,32,512]{3,2,0,1:T(8,128)(2,1)S(1)}, u32[]{:S(2)}, u32[]{:S(2)}) collective-permute-start(bf16[16,1,32,512]{3,2,0,1:T(8,128)(2,1)S(1)} %bitcast.158), channel_id=1, source_target_pairs={{0,1},{1,2},{2,3},{3,0},{4,5},{5,6},{6,7},{7,4},{8,9},{9,10},{10,1... | collective-permute-start | bytes 1572872 | tf_op jit(solution)/shard_map/ppermute | solution.py:24
  288.9 23.1 %collective-permute-start.1 = (bf16[16,1,32,512]{3,2,0,1:T(8,128)(2,1)S(1)}, bf16[16,1,32,512]{3,2,0,1:T(8,128)(2,1)S(1)}, u32[]{:S(2)}, u32[]{:S(2)}) collective-permute-start(bf16[16,1,32,512]{3,2,0,1:T(8,128)(2,1)S(1)} %bitcast.159), channel_id=1, source_target_pairs={{0,2},{1,3},{2,0},{3,1},{4,6},{5,7},{6,4},{7,5},{8,10},{9,11},{10,... | collective-permute-start | bytes 1572872 | tf_op jit(solution)/shard_map/ppermute | solution.py:24
  290.1 24.4 %collective-permute-start.2 = (bf16[16,1,32,512]{3,2,0,1:T(8,128)(2,1)S(1)}, bf16[16,1,32,512]{3,2,0,1:T(8,128)(2,1)S(1)}, u32[]{:S(2)}, u32[]{:S(2)}) collective-permute-start(bf16[16,1,32,512]{3,2,0,1:T(8,128)(2,1)S(1)} %bitcast.160), channel_id=1, source_target_pairs={{0,3},{1,0},{2,1},{3,2},{4,7},{5,4},{6,5},{7,6},{8,11},{9,8},{10,9... | collective-permute-start | bytes 1572872 | tf_op jit(solution)/shard_map/ppermute | solution.py:24
  316.7 10.5 %copy-start.9 = (bf16[2048]{0:T(1024)(128)(2,1)S(1)}, bf16[2048]{0:T(1024)(128)(2,1)}, u32[]{:S(2)}) copy-start(bf16[2048]{0:T(1024)(128)(2,1)} %param.14) | copy-start | bytes 12292
  316.7 10.6 %copy-start.3 = (bf16[256,2048]{0,1:T(8,128)(2,1)S(1)}, bf16[256,2048]{0,1:T(8,128)(2,1)}, u32[]{:S(2)}) copy-start(bf16[256,2048]{0,1:T(8,128)(2,1)} %copy-done.2) | copy-start | bytes 3145732
  316.8 61.4 %all-to-all-start.4 = ((bf16[64,1,32,512]{3,2,1,0:T(8,128)(2,1)}), bf16[64,1,32,512]{3,2,1,0:T(8,128)(2,1)}, u32[]{:S(2)}, u32[]{:S(2)}) async-start(bf16[64,1,32,512]{3,2,1,0:T(8,128)(2,1)} %bitcast.151), calls=%async_computation.4 | async-start | bytes 4194304 | tf_op jit(solution)/shard_map/all_to_all | solution.py:73
  378.2 13.7 %copy-start.1 = (bf16[704,2048]{1,0:T(8,128)(2,1)S(1)}, bf16[704,2048]{1,0:T(8,128)(2,1)}, u32[]{:S(2)}) copy-start(bf16[704,2048]{1,0:T(8,128)(2,1)} %param.21) | copy-start | bytes 8650756
Sparse Core Ops, SparseCore 0:
  10.5 115.1 all-gather.2
  127.5 64.4 all-gather.4
